TPU v7x, 512 devices: a whole 4x8x8 slice. The times are simulated.
512 devices in a mesh: section: 4 (over x_hi, core), seq: 128 (over z, y, x_lo).
Axes of the slice: x: 4 (x_hi: 2, x_lo: 2; x = x_hi * 2 + x_lo), y: 8, z: 8, core: 2. Of those that a mesh axis runs over, the one named last changes fastest.
Arguments:
- hidden: bfloat16 [2, 16384, 2688], P(None, 'seq'), may hold values from -6 to 6
- lengths: int32 [2], replicated, may hold values from 8192 to 16384, as said below
- reward_pos: int32 [2], replicated, may hold values from 8064 to 16383, as said below
- in_gain: bfloat16 [2688], P('seq'), may hold values from 0.099609375 to 1.8984375
- w_query: bfloat16 [2688, 2048], P('seq', 'section'), may hold values from -0.077151675 to 0.077151675
- w_key: bfloat16 [2688, 1024], P('seq', 'section'), may hold values from -0.077151675 to 0.077151675
- w_value: bfloat16 [2688, 1024], P('seq', 'section'), may hold values from -0.125 to 0.125
- query_gain: float32 [128], replicated, may hold values from 0.6 to 7
- key_gain: float32 [128], replicated, may hold values from 0.6 to 7
- w_out: bfloat16 [2048, 2688], P('section', 'seq'), may hold values from -0.125 to 0.125
- post_gain: bfloat16 [2688], P('seq'), may hold values from 0.099609375 to 1.8984375
- final_gain: bfloat16 [2688], P('seq'), may hold values from 0.099609375 to 1.8984375
- value_head: bfloat16 [2688], P('seq'), may hold values from -0.125 to 0.125
Outputs:
- token_values: float32 [2, 16384], P(None, 'seq')
- reward: float32 [2], replicated
Inputs may be any that keep to these rules, and one draw needn't show every extreme that they name: `lengths`: in every draw at least one micro-batch has all 16384 tokens valid. reward_pos[m] lies among the last 128 valid tokens of micro-batch m.
All inputs are finite; a program needn't handle non-finite values.
Results may differ from a plain program's by a relative error of at most 0.01.
Values may be sent and summed in bfloat16 or wider, within the bound.
No kernel may reach another device: no remote copies, remote signals or barrier semaphores. Data moves between devices by JAX's collectives and lax.ppermute only.
A program may use at most 64 MiB of HBM per device.

v0:
```python
import functools
import math
import jax
import jax.numpy as jnp
from jax import lax
from jax.sharding import Mesh
from jax.sharding import PartitionSpec as P

HD = 128
GROUP = 2
WINDOW = 1024
SEQ = ("seq_0", "seq_1", "seq_2")
norm_eps = 1e-06
query_scale = 168.0 ** (-0.5)
rope_base = 10000.0


def passed_along(array, axis, by):
    devices = lax.axis_size(axis)
    pairs = [(i, i + by) for i in range(devices) if 0 <= i + by < devices]
    return lax.ppermute(array, axis, pairs)


def sent_together(arrays, axis, dim, along):
    widths = [math.prod(a.shape[along:]) for a in arrays]
    both = jnp.concatenate(
        [a.reshape(*a.shape[:along], w) for a, w in zip(arrays, widths)], axis=along
    )
    whole = lax.all_gather(both, axis, axis=dim, tiled=True)
    tiles = jnp.split(whole, [sum(widths[:k]) for k in range(1, len(widths))], axis=along)
    return tuple((b.reshape(*whole.shape[:along], *a.shape[along:]) for a, b in zip(arrays, tiles)))


def laid_out(tiles, dim):
    tiles = jnp.moveaxis(tiles, 0, dim)
    lengths = tiles.shape
    return tiles.reshape(*lengths[:dim], lengths[dim] * lengths[dim + 1], *lengths[dim + 2 :])


def stacked_from(array, axes, turns):
    tiles = array[None]
    for k in turns:
        tiles = lax.all_gather(tiles, axes[k], axis=0, tiled=True)
    held = [lax.axis_size(axes[k]) for k in reversed(turns)]
    tiles = tiles.reshape(*held, *array.shape)
    turned = sorted(range(len(turns)), key=lambda place: turns[len(turns) - 1 - place])
    return tiles.transpose(*turned, *range(len(turns), tiles.ndim)).reshape(-1, *array.shape)


def whole_of(array, axes, turns, dim):
    return laid_out(stacked_from(array, axes, turns), dim)


def in_blocks(array, dim, devices):
    before, after = (array.shape[:dim], array.shape[dim + 1 :])
    return jnp.moveaxis(array.reshape(*before, devices, -1, *after), dim, 0)


def sent_and_summed(array, axis, dim):
    tiles = in_blocks(array, dim, lax.axis_size(axis))
    arrived = lax.all_to_all(tiles, axis, split_axis=0, concat_axis=0, tiled=True)
    return arrived.sum(axis=0)


def sent_to_all(array, axis):
    devices = lax.axis_size(axis)
    return lax.all_to_all(
        jnp.broadcast_to(array[None], (devices, *array.shape)), axis, 0, 0, tiled=True
    )


def taken_together(array, axis):
    everything = sent_to_all(array, axis)
    return jnp.sum(everything, axis=0)


def by_axis(array, axes):
    return functools.reduce(lax.psum, axes, array)


def rms_scale(values, gain_vec):
    return (
        values * lax.rsqrt(jnp.mean(values * values, axis=-1, keepdims=True) + norm_eps) * gain_vec
    )


def rotate_pairs(head_rows, positions):
    half_width = head_rows.shape[-1] // 2
    frequency = rope_base ** (
        -jnp.arange(half_width, dtype=jnp.float32) * 2.0 / head_rows.shape[-1]
    )
    angles = positions.astype(jnp.float32)[:, None] * frequency[None, :]
    target = (angles.shape[0],) + (1,) * (head_rows.ndim - 2) + (half_width,)
    cosine = jnp.cos(angles).reshape(target)
    sine_part = jnp.sin(angles).reshape(target)
    front_half = head_rows[..., :half_width]
    back_half = head_rows[..., half_width:]
    return jnp.concatenate(
        [front_half * cosine - back_half * sine_part, back_half * cosine + front_half * sine_part],
        axis=-1,
    )


def window_blocks(packed, tok_dev):
    block_count = WINDOW // tok_dev + 1
    blocks_held = [packed]
    while len(blocks_held) < block_count:
        take_count = min(len(blocks_held), block_count - len(blocks_held))
        arrived = passed_along(jnp.stack(blocks_held[:take_count]), SEQ, len(blocks_held))
        blocks_held = blocks_held + [arrived[offset] for offset in range(take_count)]
    return jnp.concatenate(blocks_held[::-1], axis=1)


def window_attention(queries, keys_all, values_all, query_pos, key_pos):
    scores = jnp.einsum("qhgd,khd->hgqk", queries, keys_all, preferred_element_type=jnp.float32)
    allowed = (
        (key_pos[None, :] <= query_pos[:, None])
        & (key_pos[None, :] > query_pos[:, None] - WINDOW)
        & (key_pos[None, :] >= 0)
    )
    scores = jnp.where(allowed[None, None], scores, -1e30)
    row_top = jnp.max(scores, axis=-1, keepdims=True)
    exponent = jnp.exp(scores - row_top)
    attn_weights = (exponent / jnp.sum(exponent, axis=-1, keepdims=True)).astype(jnp.bfloat16)
    mixed_heads = jnp.einsum(
        "hgqk,khd->qhgd", attn_weights, values_all, preferred_element_type=jnp.float32
    )
    return mixed_heads.astype(jnp.bfloat16)


def local(
    hidden,
    lengths,
    reward_pos,
    in_gain,
    w_query,
    w_key,
    w_value,
    query_gain,
    key_gain,
    w_out,
    post_gain,
    final_gain,
    value_head,
):
    micro_count, tok_dev, width = hidden.shape
    row_count = micro_count * tok_dev
    qwidth = w_query.shape[1]
    kwidth = w_key.shape[1]
    heads_here = kwidth // HD
    widened = hidden.reshape(row_count, width).astype(jnp.float32)
    inverse = lax.rsqrt(jnp.mean(widened * widened, axis=-1, keepdims=True) + norm_eps)
    seq_pos = lax.axis_index(SEQ) * tok_dev + jnp.arange(tok_dev, dtype=jnp.int32)
    positions = jnp.tile(seq_pos, micro_count)
    gain_piece, query_piece, key_piece, value_piece, post_piece, final_piece, head_piece = (
        sent_together(
            (in_gain, w_query, w_key, w_value, post_gain, final_gain, value_head), SEQ, 0, 1
        )
    )
    normed = (widened * inverse * gain_piece.astype(jnp.float32)).astype(jnp.bfloat16)
    query_acc = jnp.dot(normed, query_piece, preferred_element_type=jnp.float32)
    key_acc = jnp.dot(normed, key_piece, preferred_element_type=jnp.float32)
    value_acc = jnp.dot(normed, value_piece, preferred_element_type=jnp.float32)
    post_full = post_piece.astype(jnp.float32)
    final_full = final_piece.astype(jnp.float32)
    head_full = head_piece.astype(jnp.float32)
    folded = (query_acc, key_acc, value_acc, post_full, final_full, head_full)
    queries = folded[0].reshape(row_count, heads_here, GROUP, HD)
    queries = (rotate_pairs(rms_scale(queries, query_gain), positions) * query_scale).astype(
        jnp.bfloat16
    )
    keys_new = folded[1].reshape(row_count, heads_here, HD)
    keys_new = (
        rotate_pairs(rms_scale(keys_new, key_gain), positions)
        .astype(jnp.bfloat16)
        .reshape(row_count, kwidth)
    )
    vals_new = folded[2].astype(jnp.bfloat16)
    packed = jnp.concatenate([keys_new, vals_new], axis=1).reshape(micro_count, tok_dev, 2 * kwidth)
    window_rows = window_blocks(packed, tok_dev)
    key_pos = seq_pos[0] - WINDOW + jnp.arange(WINDOW + tok_dev, dtype=jnp.int32)
    mixed_list = []
    for micro_id in range(micro_count):
        block_queries = queries[micro_id * tok_dev : (micro_id + 1) * tok_dev]
        keys_all = window_rows[micro_id, :, :kwidth].reshape(-1, heads_here, HD)
        values_all = window_rows[micro_id, :, kwidth:].reshape(-1, heads_here, HD)
        mixed_list.append(
            window_attention(block_queries, keys_all, values_all, seq_pos, key_pos).reshape(
                tok_dev, qwidth
            )
        )
    mixed_all = jnp.concatenate(mixed_list, axis=0)
    branch = jnp.dot(
        mixed_all, whole_of(w_out, SEQ, (2, 0, 1), 1), preferred_element_type=jnp.float32
    )
    post_full, final_full, head_full = (folded[3], folded[4], folded[5])
    share_width = width // lax.axis_size("section")
    offset = lax.axis_index("section") * share_width
    share = sent_and_summed(branch, "section", 1)
    branch_sq = taken_together(jnp.sum(share * share, axis=1), "section")
    share_scale = lax.rsqrt(branch_sq / width + norm_eps)[:, None]
    post_share = lax.dynamic_slice_in_dim(post_full, offset, share_width, 0)
    updated = (
        lax.dynamic_slice_in_dim(widened, offset, share_width, 1) + share * share_scale * post_share
    ).astype(jnp.bfloat16)
    updated_wide = updated.astype(jnp.float32)
    residual_sq = taken_together(jnp.sum(updated_wide * updated_wide, axis=1), "section")
    final_share = lax.dynamic_slice_in_dim(final_full, offset, share_width, 0)
    last_rows = (
        updated_wide * lax.rsqrt(residual_sq / width + norm_eps)[:, None] * final_share
    ).astype(jnp.bfloat16)
    head_share = lax.dynamic_slice_in_dim(head_full, offset, share_width, 0).astype(jnp.bfloat16)
    raw_values = taken_together(
        jnp.dot(last_rows, head_share, preferred_element_type=jnp.float32), "section"
    )
    raw_values = raw_values.reshape(micro_count, tok_dev)
    token_values = jnp.where(seq_pos[None, :] < lengths[:, None], raw_values, 0.0)
    partial_value = jnp.sum(
        jnp.where(seq_pos[None, :] == reward_pos[:, None], token_values, 0.0), axis=1
    )
    reward = by_axis(partial_value, SEQ)
    return (token_values, reward)


def solution(mesh):
    torus = Mesh(
        mesh.devices.reshape(mesh.shape["section"], 8, 8, 2), ("section", "seq_0", "seq_1", "seq_2")
    )
    in_specs = (
        P(None, SEQ, None),
        P(),
        P(),
        P(SEQ),
        P(SEQ, "section"),
        P(SEQ, "section"),
        P(SEQ, "section"),
        P(),
        P(),
        P("section", SEQ),
        P(SEQ),
        P(SEQ),
        P(SEQ),
    )
    out_specs = (P(None, SEQ), P())
    return jax.shard_map(local, mesh=torus, in_specs=in_specs, out_specs=out_specs, check_vma=False)
```

profile of v0, /device:TPU:2, one launch (start us, length us, event | category | flops | bytes accessed | tf_op | source)
XLA Modules:
  0.0 885.2 jit_solution(14072104166463112967)
XLA Ops:
  11.8 8.6 all-gather
  20.5 28.0 %all_gather.14 = bf16[16,512,21]{1,2,0:T(8,128)(2,1)S(1)} all-gather(bf16[2,512,21]{1,2,0:T(8,128)(2,1)S(1)} %copy.153), channel_id=1, replica_groups=mesh['section'=4,'seq_0'=8,'seq_1'=8,'seq_2'=2] {'seq_0'}, dimensions={0}, use_global_device_ids=true | all-gather | bytes 387072 | tf_op jit(solution)/shard_map/all_gather | solution.py:43
  53.6 558.3 %all-gather.7.cloned.1.call-done = bf16[128,21,1028]{2,1,0:T(8,128)(2,1)} async-done(((bf16[1,21,1028]{2,1,0:T(8,128)(2,1)}), bf16[128,21,1028]{2,1,0:T(8,128)(2,1)}) %all-gather.7.cloned.1.call-update) | async-done | bytes 5526544 | tf_op jit(solution)/shard_map/all_gather | solution.py:29
  611.9 9.2 %reshape.390 = bf16[2688,1028]{1,0:T(8,128)(2,1)} reshape(bf16[128,21,1028]{2,1,0:T(8,128)(2,1)} %all-gather.7.cloned.1.call-done) | data formatting | bytes 11053056
  621.1 3.3 slice_bitcast_fusion.1
  632.2 3.1 fusion.14
  636.0 3.1 collective-permute-start.1
  641.2 17.0 %all-gather.5.cloned.1.call-done = bf16[128,512,21]{1,0,2:T(8,128)(2,1)} async-done(((bf16[16,512,21]{1,0,2:T(8,128)(2,1)}), bf16[128,512,21]{1,0,2:T(8,128)(2,1)}) %all-gather.5.cloned.1.call-update) | async-done | bytes 2752528 | tf_op jit(solution)/shard_map/all_gather | solution.py:43
  658.2 6.5 reshape.382
  664.8 6.4 copy.155
  671.1 5.4 reshape.384
  677.4 2.8 collective-permute-start.2
  680.2 5.0 slice_bitcast_fusion
  686.8 4.5 collective-permute-start
  692.9 4.5 copy.144
  699.1 3.2 multiply_reduce_fusion.2
  702.5 5.0 collective-permute-start.3
  709.5 37.9 %collective-permute-done.3 = bf16[4,2,128,512]{2,3,1,0:T(8,128)(2,1)S(1)} collective-permute-done((bf16[4,2,128,512]{2,3,1,0:T(8,128)(2,1)S(1)}, bf16[4,2,128,512]{2,3,1,0:T(8,128)(2,1)S(1)}, u32[]{:S(2)}, u32[]{:S(2)}) %collective-permute-start.3) | collective-permute-done | bytes 1048608 | tf_op jit(solution)/shard_map/ppermute | solution.py:21
  751.3 3.2 fusion.17
  757.4 3.1 fusion.18
  761.5 4.2 convolution_bitcast_fusion.2
  765.7 4.6 all-to-all-start
  770.3 3.5 fusion.68
  774.0 30.6 %all-to-all-done = f32[4,256,672]{1,2,0:T(8,128)} async-done(((f32[4,256,672]{1,2,0:T(8,128)}), f32[4,256,672]{1,2,0:T(8,128)}, u32[]{:S(2)}, u32[]{:S(2)}) %all-to-all-start) | async-done | bytes 2752544 | tf_op jit(solution)/shard_map/all_to_all | solution.py:61
  807.3 3.2 all-to-all-start.1
  811.7 4.2 all-to-all-done.1
  817.4 3.2 all-to-all-start.2
  821.7 4.2 all-to-all-done.2
  827.2 7.6 all_to_all.23
  835.6 21.5 %psum.21 = f32[2]{0:T(128)S(1)} all-reduce(f32[2]{0:T(128)S(1)} %get-tuple-element.2), channel_id=1, replica_groups=mesh['section'=4,'seq_0'=8,'seq_1'=8,'seq_2'=2] {'seq_0'}, use_global_device_ids=true, to_apply=%region_14.15 | all-reduce | flops 2 | bytes 16 | tf_op jit(solution)/shard_map/psum | solution.py:78
  857.2 15.8 %psum.22 = f32[2]{0:T(128)S(1)} all-reduce(f32[2]{0:T(128)S(1)} %psum.21), channel_id=1, replica_groups=mesh['section'=4,'seq_0'=8,'seq_1'=8,'seq_2'=2] {'seq_1'}, use_global_device_ids=true, to_apply=%region_15.16 | all-reduce | flops 2 | bytes 16 | tf_op jit(solution)/shard_map/psum | solution.py:78
  872.9 5.4 psum.23
  (118 shorter events, 44.2 us)
Async XLA Ops:
  7.2 604.7 %all-gather.7.cloned.1.call-start = ((), (), s32[]{:S(2)}) async-start(), calls=%async_computation.5 | async-start | bytes 7133184 | tf_op jit(solution)/shard_map/all_gather | solution.py:29
  11.8 646.4 %all-gather.5.cloned.1.call-start = ((), (), s32[]{:S(2)}) async-start(), calls=%async_computation.4 | async-start | bytes 3096576 | tf_op jit(solution)/shard_map/all_gather | solution.py:43
  53.6 578.4 %copy-start.8 = (f32[256,64]{0,1:T(8,128)}, f32[256,64]{0,1:T(8,128)S(1)}, u32[]{:S(2)}) copy-start(f32[256,64]{0,1:T(8,128)S(1)} %get-tuple-element.17) | copy-start | bytes 196612
  53.6 578.4 %copy-start.10 = (f32[256,64]{0,1:T(8,128)}, f32[256,64]{0,1:T(8,128)S(1)}, u32[]{:S(2)}) copy-start(f32[256,64]{0,1:T(8,128)S(1)} %get-tuple-element.18) | copy-start | bytes 196612
  627.0 4.3 copy-start.5
  628.5 3.4 copy-start.16
  630.2 1.1 copy-start.4
  632.1 3.2 copy-start.6
  632.2 44.4 %copy-start = (bf16[1,2,128,256]{2,3,1,0:T(8,128)(2,1)}, bf16[1,2,128,256]{2,3,1,0:T(8,128)(2,1)S(1)}, u32[]{:S(2)}) copy-start(bf16[1,2,128,256]{2,3,1,0:T(8,128)(2,1)S(1)} %copy.140) | copy-start | bytes 393220
  635.3 0.7 copy-start.7
  635.9 40.6 %copy-start.2 = (bf16[1,2,128,256]{2,3,1,0:T(8,128)(2,1)}, bf16[1,2,128,256]{2,3,1,0:T(8,128)(2,1)S(1)}, u32[]{:S(2)}) copy-start(bf16[1,2,128,256]{2,3,1,0:T(8,128)(2,1)S(1)} %copy.141) | copy-start | bytes 393220
  635.9 28.8 %copy-start.14 = (bf16[1,2,128,512]{2,3,1,0:T(8,128)(2,1)}, bf16[1,2,128,512]{2,3,1,0:T(8,128)(2,1)S(1)}, u32[]{:S(2)}) copy-start(bf16[1,2,128,512]{2,3,1,0:T(8,128)(2,1)S(1)} %pad_maximum_fusion.2) | copy-start | bytes 786436
  636.0 40.6 %collective-permute-start.1 = (bf16[1,2,128,512]{2,3,1,0:T(8,128)(2,1)S(1)}, bf16[1,2,128,512]{2,3,1,0:T(8,128)(2,1)S(1)}, u32[]{:S(2)}, u32[]{:S(2)}) collective-permute-start(bf16[1,2,128,512]{2,3,1,0:T(8,128)(2,1)S(1)} %pad_maximum_fusion.2), channel_id=1, source_target_pairs={{0,1},{1,2},{2,3},{3,4},{4,5},{5,6},{6,7},{7,8},{8,9},{9,10},{10,1... | collective-permute-start | bytes 786440 | tf_op jit(solution)/shard_map/ppermute | solution.py:21
  677.4 25.0 %collective-permute-start.2 = (bf16[2,2,128,512]{2,3,1,0:T(8,128)(2,1)}, bf16[2,2,128,512]{2,3,1,0:T(8,128)(2,1)S(1)}, u32[]{:S(2)}, u32[]{:S(2)}) collective-permute-start(bf16[2,2,128,512]{2,3,1,0:T(8,128)(2,1)} %pad_maximum_fusion.1), channel_id=1, source_target_pairs={{0,2},{1,3},{2,4},{3,5},{4,6},{5,7},{6,8},{7,9},{8,10},{9,11},{10,... | collective-permute-start | bytes 1572872 | tf_op jit(solution)/shard_map/ppermute | solution.py:21
  686.8 21.7 %collective-permute-start = (bf16[1,2,128,512]{2,3,1,0:T(8,128)(2,1)}, bf16[1,2,128,512]{2,3,1,0:T(8,128)(2,1)}, u32[]{:S(2)}, u32[]{:S(2)}) collective-permute-start(bf16[1,2,128,512]{2,3,1,0:T(8,128)(2,1)} %copy-done.14), channel_id=1, source_target_pairs={{0,8},{1,9},{2,10},{3,11},{4,12},{5,13},{6,14},{7,15},{8,16},{9,17... | collective-permute-start | bytes 786440 | tf_op jit(solution)/shard_map/ppermute | solution.py:21
  699.1 3.2 copy-start.1
  699.1 3.2 copy-start.3
  699.1 8.4 copy-start.17
  702.3 5.3 copy-start.9
  702.3 5.3 copy-start.11
  702.5 44.9 %collective-permute-start.3 = (bf16[4,2,128,512]{2,3,1,0:T(8,128)(2,1)S(1)}, bf16[4,2,128,512]{2,3,1,0:T(8,128)(2,1)S(1)}, u32[]{:S(2)}, u32[]{:S(2)}) collective-permute-start(bf16[4,2,128,512]{2,3,1,0:T(8,128)(2,1)S(1)} %pad_maximum_fusion), channel_id=1, source_target_pairs={{0,4},{1,5},{2,6},{3,7},{4,8},{5,9},{6,10},{7,11},{8,12},{9,13},{1... | collective-permute-start | bytes 3145736 | tf_op jit(solution)/shard_map/ppermute | solution.py:21
  707.8 40.1 %copy-start.12 = (bf16[2,128,256]{1,2,0:T(8,128)(2,1)S(1)}, bf16[2,128,256]{1,2,0:T(8,128)(2,1)}, u32[]{:S(2)}) copy-start(bf16[2,128,256]{1,2,0:T(8,128)(2,1)} %copy.142) | copy-start | bytes 393220
  707.8 40.1 %copy-start.13 = (bf16[2,128,256]{1,2,0:T(8,128)(2,1)S(1)}, bf16[2,128,256]{1,2,0:T(8,128)(2,1)}, u32[]{:S(2)}) copy-start(bf16[2,128,256]{1,2,0:T(8,128)(2,1)} %copy.143) | copy-start | bytes 393220
  748.0 1.3 copy-start.15
  765.7 38.8 %all-to-all-start = ((f32[4,256,672]{1,2,0:T(8,128)}), f32[4,256,672]{1,2,0:T(8,128)}, u32[]{:S(2)}, u32[]{:S(2)}) async-start(f32[4,256,672]{1,2,0:T(8,128)} %convolution_bitcast_fusion.2), calls=%async_computation | async-start | bytes 5505024 | tf_op jit(solution)/shard_map/all_to_all | solution.py:61
  806.6 28.2 %copy-start.18 = (s32[2]{0:T(128)S(1)}, s32[2]{0:T(128)}, u32[]{:S(2)}) copy-start(s32[2]{0:T(128)} %param.15) | copy-start | bytes 28
  806.6 28.2 %copy-start.19 = (s32[2]{0:T(128)S(1)}, s32[2]{0:T(128)}, u32[]{:S(2)}) copy-start(s32[2]{0:T(128)} %param.14) | copy-start | bytes 28
  807.3 8.5 all-to-all-start.1
  817.4 8.5 all-to-all-start.2
Sparse Core Ops, SparseCore 0:
  11.9 599.9 all-gather.6
  614.0 44.1 all-gather.4
where the time goes:
time: 887 us; the launch traced here: 885 us
  waiting for transfers between devices  652 us (74%)
  blocking collectives  87 us (10%)
  local copies, waits for them, and re-layouts  66.1 us (7%)
  starting transfers between devices  26.7 us (3%)
  matrix products  22.5 us (3%)
  other arithmetic  16.2 us (2%)
  between operations  14.6 us (2%)
    all_gather x1, waiting for transfers between devices, sent_together(): whole = lax.all_gather(both, axis, axis=dim, tiled=True)  558 us
    psum x3, blocking collectives, by_axis(): return functools.reduce(lax.psum, axes, array)  42.8 us
    ppermute x4, waiting for transfers between devices, passed_along(): return lax.ppermute(array, axis, pairs)  37.9 us
    all_gather x2, blocking collectives, stacked_from(): tiles = lax.all_gather(tiles, axes[k], axis=0, tiled=True)  36.6 us
    all_to_all x1, waiting for transfers between devices, sent_and_summed(): lax.all_to_all(tiles, axis, split_axis=0, concat_axis=0, tiled=True)  30.6 us
  transfers between devices with their start and end apart: 9, of which 6 were waited for; matrix products, arithmetic and copies ran while one was open for 8% of the time, Pallas kernels for 0%

commit v1 on v0

--- a/solution.py
+++ b/solution.py
@@ -40,7 +40,11 @@
 def stacked_from(array, axes, turns):
     tiles = array[None]
     for k in turns:
-        tiles = lax.all_gather(tiles, axes[k], axis=0, tiled=True)
+        matrix = axes[k]
+        spare = lax.axis_size(matrix)
+        o_now = jnp.stack([tiles] * spare, axis=0)
+        mixed_arr = lax.all_to_all(o_now, matrix, 0, 0)
+        tiles = jnp.concatenate(mixed_arr, axis=0)
     held = [lax.axis_size(axes[k]) for k in reversed(turns)]
     tiles = tiles.reshape(*held, *array.shape)
     turned = sorted(range(len(turns)), key=lambda place: turns[len(turns) - 1 - place])

time: 887 us -> 867 us (0.977)
  blocking collectives: 87 us -> 68.6 us
  waiting for transfers between devices: 652 us -> 637 us
  local copies, waits for them, and re-layouts: 66.1 us -> 75.2 us
    all_gather x2 -> x0, blocking collectives: 36.6 us -> none  [stacked_from(): tiles = lax.all_gather(tiles, axes[k], axis=0, tiled=True)]
    ppermute x4, waiting for transfers between devices: 37.9 us -> 15.8 us  [passed_along(): return lax.ppermute(array, axis, pairs)]
    all_gather x1 -> x0, waiting for transfers between devices: 17 us -> none  [stacked_from(): tiles = lax.all_gather(tiles, axes[k], axis=0, tiled=True)]
    all_to_all x0 -> x2, waiting for transfers between devices: none -> 13 us  [stacked_from(): mixed_arr = lax.all_to_all(o_now, matrix, 0, 0)]
    all_to_all x0 -> x2, starting transfers between devices: none -> 11.3 us  [stacked_from(): mixed_arr = lax.all_to_all(o_now, matrix, 0, 0)]
    all_gather x1, waiting for transfers between devices: 558 us -> 569 us  [sent_together(): whole = lax.all_gather(both, axis, axis=dim, tiled=True)]
    all_to_all x0 -> x1, blocking collectives: none -> 10.3 us  [stacked_from(): mixed_arr = lax.all_to_all(o_now, matrix, 0, 0)]
  transfers between devices with their start and end apart: 9 -> 10, of which waited for: 6 -> 6; matrix products, arithmetic and copies ran while one was open for 8% -> 10% of each run, Pallas kernels for 0% -> 0%
where the time goes in v1:
time: 867 us; the launch traced here: 865 us
  waiting for transfers between devices  637 us (73%)
  local copies, waits for them, and re-layouts  75.2 us (9%)
  blocking collectives  68.6 us (8%)
  starting transfers between devices  30.6 us (4%)
  matrix products  22.5 us (3%)
  other arithmetic  17 us (2%)
  between operations  14.6 us (2%)
    all_gather x1, waiting for transfers between devices, sent_together(): whole = lax.all_gather(both, axis, axis=dim, tiled=True)  569 us
    psum x3, blocking collectives, by_axis(): return functools.reduce(lax.psum, axes, array)  50.7 us
    all_to_all x1, waiting for transfers between devices, sent_and_summed(): lax.all_to_all(tiles, axis, split_axis=0, concat_axis=0, tiled=True)  30.6 us
  transfers between devices with their start and end apart: 10, of which 6 were waited for; matrix products, arithmetic and copies ran while one was open for 10% of the time, Pallas kernels for 0%

profile of v1, /device:TPU:2, one launch (start us, length us, event | category | flops | bytes accessed | tf_op | source)
XLA Modules:
  0.0 865.0 jit_solution(4190547792489884671)
XLA Ops:
  12.6 10.3 %all_to_all.38 = bf16[2,1,512,21]{2,3,1,0:T(8,128)(2,1)S(1)} all-to-all(bf16[2,1,512,21]{2,3,1,0:T(8,128)(2,1)S(1)} %pad_maximum_fusion.3), channel_id=1, replica_groups=mesh['section'=4,'seq_0'=8,'seq_1'=8,'seq_2'=2] {'seq_2'}, dimensions={0} | all-to-all | bytes 86016 | tf_op jit(solution)/shard_map/all_to_all | solution.py:46
  23.8 5.2 all-to-all-start.1
  29.5 13.0 %all-to-all-done.1 = bf16[8,2,512,21]{2,1,3,0:T(2,128)(2,1)S(1)} async-done(((bf16[8,2,512,21]{2,1,3,0:T(2,128)(2,1)}), bf16[8,2,512,21]{2,1,3,0:T(2,128)(2,1)S(1)}, u32[]{:S(2)}, u32[]{:S(2)}) %all-to-all-start.1) | async-done | bytes 344096 | tf_op jit(solution)/shard_map/all_to_all | solution.py:46
  44.9 6.1 all-to-all-start.2
  54.8 568.7 %all-gather.3.cloned.1.call-done = bf16[128,21,1028]{2,1,0:T(8,128)(2,1)} async-done(((bf16[1,21,1028]{2,1,0:T(8,128)(2,1)}), bf16[128,21,1028]{2,1,0:T(8,128)(2,1)}) %all-gather.3.cloned.1.call-update) | async-done | bytes 5526544 | tf_op jit(solution)/shard_map/all_gather | solution.py:29
  623.5 9.2 %reshape.389 = bf16[2688,1028]{1,0:T(8,128)(2,1)} reshape(bf16[128,21,1028]{2,1,0:T(8,128)(2,1)} %all-gather.3.cloned.1.call-done) | data formatting | bytes 11053056
  632.7 3.3 slice_bitcast_fusion.1
  643.8 3.1 fusion.14
  651.8 3.3 copy.185
  655.1 4.4 copy.186
  659.5 6.8 reshape.383
  666.3 5.0 copy.187
  671.3 5.4 reshape.384
  678.8 5.0 slice_bitcast_fusion
  689.0 4.5 copy.174
  695.2 3.2 multiply_reduce_fusion.2
  698.6 2.8 collective-permute-start.3
  703.4 15.8 %collective-permute-done.3 = bf16[4,2,128,512]{2,3,1,0:T(8,128)(2,1)S(1)} collective-permute-done((bf16[4,2,128,512]{2,3,1,0:T(8,128)(2,1)S(1)}, bf16[4,2,128,512]{2,3,1,0:T(8,128)(2,1)S(1)}, u32[]{:S(2)}, u32[]{:S(2)}) %collective-permute-start.3) | collective-permute-done | bytes 1048608 | tf_op jit(solution)/shard_map/ppermute | solution.py:21
  723.1 3.2 fusion.17
  729.2 3.1 fusion.18
  733.3 4.2 convolution_bitcast_fusion.2
  737.5 4.6 all-to-all-start.3
  742.1 3.5 fusion.68
  745.8 30.6 %all-to-all-done.3 = f32[4,256,672]{1,2,0:T(8,128)} async-done(((f32[4,256,672]{1,2,0:T(8,128)}), f32[4,256,672]{1,2,0:T(8,128)}, u32[]{:S(2)}, u32[]{:S(2)}) %all-to-all-start.3) | async-done | bytes 2752544 | tf_op jit(solution)/shard_map/all_to_all | solution.py:65
  779.1 3.2 all-to-all-start.4
  783.5 4.2 all-to-all-done.4
  789.2 3.2 all-to-all-start.5
  793.5 4.2 all-to-all-done.5
  799.0 7.6 all_to_all.39
  807.4 28.0 %psum.21 = f32[2]{0:T(128)S(1)} all-reduce(f32[2]{0:T(128)S(1)} %get-tuple-element.2), channel_id=1, replica_groups=mesh['section'=4,'seq_0'=8,'seq_1'=8,'seq_2'=2] {'seq_0'}, use_global_device_ids=true, to_apply=%region_14.15 | all-reduce | flops 2 | bytes 16 | tf_op jit(solution)/shard_map/psum | solution.py:82
  835.4 17.3 %psum.22 = f32[2]{0:T(128)S(1)} all-reduce(f32[2]{0:T(128)S(1)} %psum.21), channel_id=1, replica_groups=mesh['section'=4,'seq_0'=8,'seq_1'=8,'seq_2'=2] {'seq_1'}, use_global_device_ids=true, to_apply=%region_15.16 | all-reduce | flops 2 | bytes 16 | tf_op jit(solution)/shard_map/psum | solution.py:82
  852.7 5.4 psum.23
  (123 shorter events, 52.8 us)
Async XLA Ops:
  7.2 616.3 %all-gather.3.cloned.1.call-start = ((), (), s32[]{:S(2)}) async-start(), calls=%async_computation.7 | async-start | bytes 7133184 | tf_op jit(solution)/shard_map/all_gather | solution.py:29
  23.8 18.7 %all-to-all-start.1 = ((bf16[8,2,512,21]{2,1,3,0:T(2,128)(2,1)}), bf16[8,2,512,21]{2,1,3,0:T(2,128)(2,1)S(1)}, u32[]{:S(2)}, u32[]{:S(2)}) async-start(bf16[8,2,512,21]{2,1,3,0:T(2,128)(2,1)} %stack.19), calls=%async_computation.1 | async-start | bytes 688128 | tf_op jit(solution)/shard_map/all_to_all | solution.py:46
  44.9 606.9 %all-to-all-start.2 = ((bf16[8,16,512,21]{2,1,3,0:T(8,128)(2,1)}), bf16[8,16,512,21]{2,1,3,0:T(8,128)(2,1)}, u32[]{:S(2)}, u32[]{:S(2)}) async-start(bf16[8,16,512,21]{2,1,3,0:T(8,128)(2,1)} %stack.20), calls=%async_computation.2 | async-start | bytes 5505024 | tf_op jit(solution)/shard_map/all_to_all | solution.py:46
  54.7 588.8 %copy-start.8 = (f32[256,64]{0,1:T(8,128)}, f32[256,64]{0,1:T(8,128)S(1)}, u32[]{:S(2)}) copy-start(f32[256,64]{0,1:T(8,128)S(1)} %get-tuple-element.17) | copy-start | bytes 196612
  54.8 588.8 %copy-start.10 = (f32[256,64]{0,1:T(8,128)}, f32[256,64]{0,1:T(8,128)S(1)}, u32[]{:S(2)}) copy-start(f32[256,64]{0,1:T(8,128)S(1)} %get-tuple-element.18) | copy-start | bytes 196612
  638.6 4.3 copy-start.5
  640.0 3.4 copy-start.16
  641.8 1.1 copy-start.4
  643.7 3.2 copy-start.6
  643.7 32.9 %copy-start = (bf16[1,2,128,256]{2,3,1,0:T(8,128)(2,1)}, bf16[1,2,128,256]{2,3,1,0:T(8,128)(2,1)S(1)}, u32[]{:S(2)}) copy-start(bf16[1,2,128,256]{2,3,1,0:T(8,128)(2,1)S(1)} %copy.170) | copy-start | bytes 393220
  646.8 0.7 copy-start.7
  647.5 29.2 %copy-start.2 = (bf16[1,2,128,256]{2,3,1,0:T(8,128)(2,1)}, bf16[1,2,128,256]{2,3,1,0:T(8,128)(2,1)S(1)}, u32[]{:S(2)}) copy-start(bf16[1,2,128,256]{2,3,1,0:T(8,128)(2,1)S(1)} %copy.171) | copy-start | bytes 393220
  647.5 7.6 copy-start.14
  647.5 29.2 %collective-permute-start.1 = (bf16[1,2,128,512]{2,3,1,0:T(8,128)(2,1)S(1)}, bf16[1,2,128,512]{2,3,1,0:T(8,128)(2,1)S(1)}, u32[]{:S(2)}, u32[]{:S(2)}) collective-permute-start(bf16[1,2,128,512]{2,3,1,0:T(8,128)(2,1)S(1)} %pad_maximum_fusion.2), channel_id=1, source_target_pairs={{0,1},{1,2},{2,3},{3,4},{4,5},{5,6},{6,7},{7,8},{8,9},{9,10},{10,1... | collective-permute-start | bytes 786440 | tf_op jit(solution)/shard_map/ppermute | solution.py:21
  677.5 20.9 %collective-permute-start.2 = (bf16[2,2,128,512]{2,3,1,0:T(8,128)(2,1)}, bf16[2,2,128,512]{2,3,1,0:T(8,128)(2,1)S(1)}, u32[]{:S(2)}, u32[]{:S(2)}) collective-permute-start(bf16[2,2,128,512]{2,3,1,0:T(8,128)(2,1)} %pad_maximum_fusion.1), channel_id=1, source_target_pairs={{0,2},{1,3},{2,4},{3,5},{4,6},{5,7},{6,8},{7,9},{8,10},{9,11},{10,... | collective-permute-start | bytes 1572872 | tf_op jit(solution)/shard_map/ppermute | solution.py:21
  685.5 16.9 %collective-permute-start = (bf16[1,2,128,512]{2,3,1,0:T(8,128)(2,1)}, bf16[1,2,128,512]{2,3,1,0:T(8,128)(2,1)}, u32[]{:S(2)}, u32[]{:S(2)}) collective-permute-start(bf16[1,2,128,512]{2,3,1,0:T(8,128)(2,1)} %copy-done.14), channel_id=1, source_target_pairs={{0,8},{1,9},{2,10},{3,11},{4,12},{5,13},{6,14},{7,15},{8,16},{9,17... | collective-permute-start | bytes 786440 | tf_op jit(solution)/shard_map/ppermute | solution.py:21
  695.2 3.2 copy-start.1
  695.2 3.2 copy-start.3
  695.2 6.2 copy-start.17
  698.4 3.1 copy-start.9
  698.4 3.1 copy-start.11
  698.6 20.6 %collective-permute-start.3 = (bf16[4,2,128,512]{2,3,1,0:T(8,128)(2,1)S(1)}, bf16[4,2,128,512]{2,3,1,0:T(8,128)(2,1)S(1)}, u32[]{:S(2)}, u32[]{:S(2)}) collective-permute-start(bf16[4,2,128,512]{2,3,1,0:T(8,128)(2,1)S(1)} %pad_maximum_fusion), channel_id=1, source_target_pairs={{0,4},{1,5},{2,6},{3,7},{4,8},{5,9},{6,10},{7,11},{8,12},{9,13},{1... | collective-permute-start | bytes 3145736 | tf_op jit(solution)/shard_map/ppermute | solution.py:21
  701.6 18.1 %copy-start.12 = (bf16[2,128,256]{1,2,0:T(8,128)(2,1)S(1)}, bf16[2,128,256]{1,2,0:T(8,128)(2,1)}, u32[]{:S(2)}) copy-start(bf16[2,128,256]{1,2,0:T(8,128)(2,1)} %copy.172) | copy-start | bytes 393220
  701.6 18.1 %copy-start.13 = (bf16[2,128,256]{1,2,0:T(8,128)(2,1)S(1)}, bf16[2,128,256]{1,2,0:T(8,128)(2,1)}, u32[]{:S(2)}) copy-start(bf16[2,128,256]{1,2,0:T(8,128)(2,1)} %copy.173) | copy-start | bytes 393220
  719.8 1.3 copy-start.15
  737.5 38.8 %all-to-all-start.3 = ((f32[4,256,672]{1,2,0:T(8,128)}), f32[4,256,672]{1,2,0:T(8,128)}, u32[]{:S(2)}, u32[]{:S(2)}) async-start(f32[4,256,672]{1,2,0:T(8,128)} %convolution_bitcast_fusion.2), calls=%async_computation.3 | async-start | bytes 5505024 | tf_op jit(solution)/shard_map/all_to_all | solution.py:65
  778.4 28.2 %copy-start.18 = (s32[2]{0:T(128)S(1)}, s32[2]{0:T(128)}, u32[]{:S(2)}) copy-start(s32[2]{0:T(128)} %param.15) | copy-start | bytes 28
  778.4 28.2 %copy-start.19 = (s32[2]{0:T(128)S(1)}, s32[2]{0:T(128)}, u32[]{:S(2)}) copy-start(s32[2]{0:T(128)} %param.14) | copy-start | bytes 28
  779.1 8.5 all-to-all-start.4
  789.2 8.5 all-to-all-start.5
Sparse Core Ops, SparseCore 0:
  11.9 611.5 all-gather.2
